TPU v7x, 32 devices: a whole 2x2x4 slice. The times are simulated.
32 devices in a mesh: row: 8 (over z, x), mem: 2 (over core), lev: 2 (over y).
Axes of the slice: x: 2, y: 2, z: 4, core: 2. Of those that a mesh axis runs over, the one named last changes fastest.
Arguments:
- control_fields: bfloat16 [4, 6, 256, 2048], P('mem', 'lev', 'row'), may hold values from -6 to 6
- perturbations: bfloat16 [3, 4, 6, 256, 2048], P(None, 'mem', 'lev', 'row'), may hold values from -3 to 3
- column_taper: bfloat16 [2048, 2048], P('row'), may hold values from -1 to 2, as said below
- row_taper: bfloat16 [256, 256], P('row'), may hold values from -1 to 2, as said below
- courant_numbers: float32 [3, 6, 256, 2048], P(None, 'lev', 'row', 'mem'), may hold values from -0.3 to 0.3
- tracer_slope: float32 [2, 6, 256, 2048], P(None, 'lev', 'row', 'mem'), may hold values from -3 to 3
Outputs:
- increment: float32 [3, 6, 256, 2048], P(None, 'lev', 'row', 'mem')
Inputs may be any that keep to these rules, and one draw needn't show every extreme that they name: `column_taper`: A square matrix. `row_taper`: A square matrix.
All inputs are finite; a program needn't handle non-finite values.
Results may differ from a plain program's by a relative error of at most 0.0048.
Values may be sent and summed in bfloat16 or wider, within the bound.
A program may use at most 64 MiB of HBM per device.

v0:
```python
import jax
import jax.numpy as jnp
from jax import lax
from jax.sharding import PartitionSpec as P

STEPS = 4


def extended(block, sides, width):
    for axis, dim in sides:
        count = lax.axis_size(axis)
        forward = [(i, i + 1) for i in range(count - 1)]
        backward = [(target, source) for source, target in forward]
        low = lax.ppermute(
            lax.slice_in_dim(block, block.shape[dim] - width, None, axis=dim), axis, forward
        )
        high = lax.ppermute(lax.slice_in_dim(block, 0, width, axis=dim), axis, backward)
        block = jnp.concatenate([low, block, high], axis=dim)
    return block


def upwind(middle, behind, forward, velocity):
    return jnp.maximum(velocity, 0.0) * (middle - behind) + jnp.minimum(velocity, 0.0) * (
        forward - middle
    )


def advance(present, courant_numbers, tracer_slope, padded):
    middle = padded[:, 1:-1, 1:-1, 1:-1]
    change = upwind(
        middle, padded[:, :-2, 1:-1, 1:-1], padded[:, 2:, 1:-1, 1:-1], courant_numbers[0]
    )
    change = change + upwind(
        middle, padded[:, 1:-1, :-2, 1:-1], padded[:, 1:-1, 2:, 1:-1], courant_numbers[1]
    )
    change = change + upwind(
        middle, padded[:, 1:-1, 1:-1, :-2], padded[:, 1:-1, 1:-1, 2:], courant_numbers[2]
    )
    shifted = present - change
    source = present[0] * tracer_slope[0] + present[1] * tracer_slope[1]
    return jnp.concatenate([shifted[:2], shifted[2:] - source[None]], axis=0)


def on_device(
    control_fields, perturbations, column_taper, row_taper, courant_numbers, tracer_slope
):
    member_count, level_count, row_count, column_count = control_fields.shape
    field_count = member_count * level_count
    flattened = control_fields.reshape(field_count * row_count, column_count)
    block_width = column_count // lax.axis_size("mem")
    own_block = lax.dynamic_slice_in_dim(
        column_taper, lax.axis_index("mem") * block_width, block_width, 1
    )
    column_block = lax.all_gather(own_block, "row", axis=0, tiled=True)
    first_pass = jnp.dot(
        flattened,
        lax.all_gather(column_block, "mem", axis=1, tiled=True),
        preferred_element_type=jnp.float32,
    )
    first_pass = first_pass.astype(jnp.bfloat16).reshape(field_count, row_count, column_count)
    row_whole = lax.all_gather(row_taper, "row", axis=0, tiled=True)
    tapered = jnp.einsum(
        "ij,fjc->fic",
        row_whole,
        lax.all_to_all(first_pass, "row", split_axis=2, concat_axis=1, tiled=True),
        preferred_element_type=jnp.float32,
    )
    localized = lax.all_to_all(
        tapered.astype(jnp.bfloat16), "row", split_axis=1, concat_axis=2, tiled=True
    )
    localized = localized.reshape(member_count, level_count, row_count, column_count)
    weighted = jnp.einsum(
        "kmlrc,mlrc->klrc", perturbations, localized, preferred_element_type=jnp.float32
    )
    summed = lax.psum(weighted, "mem")
    own_columns = column_count // lax.axis_size("mem")
    margin = STEPS
    widened = jnp.pad(summed, ((0, 0), (0, 0), (0, 0), (margin, margin)))
    present = lax.dynamic_slice_in_dim(
        widened, lax.axis_index("mem") * own_columns, own_columns + 2 * margin, 3
    )
    background = jnp.concatenate([courant_numbers, tracer_slope], axis=0)
    background = extended(background, (("mem", 3),), margin - 1)
    background = jnp.pad(background, ((0, 0), (0, 0), (0, 0), (1, 1)))
    courant_near = background[:3]
    slope_near = background[3:]
    for advect_step in range(STEPS):
        padded = extended(present, (("row", 2), ("lev", 1)), 1)
        padded = jnp.pad(padded, ((0, 0), (0, 0), (0, 0), (1, 1)))
        present = advance(present, courant_near, slope_near, padded)
    return present[:, :, :, margin : margin + own_columns]


def solution(mesh):
    placed = (
        P("mem", "lev", "row", None),
        P(None, "mem", "lev", "row", None),
        P("row", None),
        P("row", None),
        P(None, "lev", "row", "mem"),
        P(None, "lev", "row", "mem"),
    )
    return jax.shard_map(
        on_device,
        mesh=mesh,
        in_specs=placed,
        out_specs=P(None, "lev", "row", "mem"),
        check_vma=False,
    )
```

profile of v0, /device:TPU:0, one launch (start us, length us, event | category | flops | bytes accessed | tf_op | source)
XLA Modules:
  0.0 356.1 jit_solution(13105754108425344147)
XLA Ops:
  8.7 76.3 %all-gather.3.cloned.1.call-done = bf16[2048,1024]{1,0:T(8,128)(2,1)} async-done(((bf16[256,1024]{1,0:T(8,128)(2,1)}), bf16[2048,1024]{1,0:T(8,128)(2,1)}) %all-gather.3.cloned.1.call-update) | async-done | bytes 4194320 | tf_op jit(solution)/shard_map/all_gather | solution.py:54
  85.0 19.9 %all-gather.5.cloned.1.call-done = bf16[2048,2048]{1,0:T(8,128)(2,1)} async-done(((bf16[2048,1024]{1,0:T(8,128)(2,1)}), bf16[2048,2048]{1,0:T(8,128)(2,1)}) %all-gather.5.cloned.1.call-update) | async-done | bytes 8388624 | tf_op jit(solution)/shard_map/all_gather | solution.py:57
  105.0 5.2 %convolution_convert_fusion = bf16[2048,192]{0,1:T(8,128)(2,1)S(1)} fusion(bf16[192,2048]{1,0:T(8,128)(2,1)S(1)} %bitcast.47, bf16[2048,2048]{1,0:T(8,128)(2,1)} %all-gather.5.cloned.1.call-done), kind=kOutput, calls=%fused_computation.23 | convolution fusion | flops 1611005952 | bytes 9961472 | tf_op jit(solution)/shard_map/dot_general | solution.py:55
  110.2 4.2 %copy.15 = bf16[6,32,2048]{1,0,2:T(8,128)(2,1)} copy(bf16[6,32,2048]{2,1,0:T(8,128)(2,1)S(1)} %bitcast.46) | data formatting | bytes 1572864 | tf_op jit(solution)/shard_map/reshape | solution.py:60
  114.3 5.7 %reshape.16 = bf16[8,2,24576]{2,1,0:T(2,128)(2,1)} reshape(bf16[2048,6,32]{2,1,0:T(8,128)(2,1)} %bitcast.41) | data formatting | bytes 1572864
  120.0 5.9 %all-to-all-start = ((bf16[8,2,24576]{2,1,0:T(2,128)(2,1)}), bf16[8,2,24576]{2,1,0:T(2,128)(2,1)S(1)}, u32[]{:S(2)}, u32[]{:S(2)}) async-start(bf16[8,2,24576]{2,1,0:T(2,128)(2,1)} %reshape.16), calls=%async_computation | async-start | bytes 1572864 | tf_op jit(solution)/shard_map/all_to_all | solution.py:65
  126.0 41.8 %all_gather.11 = bf16[256,256]{1,0:T(8,128)(2,1)S(1)} all-gather(bf16[32,256]{1,0:T(8,128)(2,1)S(1)} %copy-done.9), channel_id=1, replica_groups=mesh['row'=8,'mem'=2,'lev'=2] {'row'}, dimensions={0}, use_global_device_ids=true | all-gather | bytes 147456 | tf_op jit(solution)/shard_map/all_gather | solution.py:61
  167.8 4.1 %reshape.17 = bf16[2048,6,32]{2,1,0:T(8,128)(2,1)} reshape(bf16[8,2,24576]{2,1,0:T(2,128)(2,1)S(1)} %all-to-all-done) | data formatting | bytes 1572864
  171.9 4.1 %copy.17 = bf16[6,8,32,256]{3,2,1,0:T(8,128)(2,1)S(1)} copy(bf16[6,8,32,256]{2,0,3,1:T(8,128)(2,1)} %bitcast.42) | data formatting | bytes 1572864 | tf_op jit(solution)/shard_map/all_to_all | solution.py:65
  177.4 22.4 %all_to_all.33 = bf16[6,256,256]{2,0,1:T(8,128)(2,1)S(1)} all-to-all(bf16[6,256,256]{2,0,1:T(8,128)(2,1)S(1)} %copy.19), channel_id=1, replica_groups=mesh['row'=8,'mem'=2,'lev'=2] {'row'}, dimensions={1} | all-to-all | bytes 1572864 | tf_op jit(solution)/shard_map/all_to_all | solution.py:68
  205.9 19.7 %all-reduce.8.cloned.1.call-done = f32[3,3,32,2048]{3,2,1,0:T(8,128)} async-done(((f32[3,3,32,2048]{3,2,1,0:T(8,128)}), f32[3,3,32,2048]{3,2,1,0:T(8,128)}) %all-reduce.8.cloned.1.call-update) | async-done | bytes 2359312 | tf_op jit(solution)/shard_map/psum | solution.py:75
  232.5 4.2 %collective-permute-done.3 = f32[3,3,1,1032]{3,2,1,0:T(1,128)S(1)} collective-permute-done((f32[3,3,1,1032]{3,2,1,0:T(1,128)S(1)}, f32[3,3,1,1032]{3,2,1,0:T(1,128)S(1)}, u32[]{:S(2)}, u32[]{:S(2)}) %collective-permute-start.3) | collective-permute-done | bytes 37184 | tf_op jit(solution)/shard_map/ppermute | solution.py:17
  237.8 4.2 %collective-permute-start.4 = (f32[3,1,34,1032]{3,2,1,0:T(8,128)}, f32[3,1,34,1032]{3,2,1,0:T(8,128)}, u32[]{:S(2)}, u32[]{:S(2)}) collective-permute-start(f32[3,1,34,1032]{3,2,1,0:T(8,128)} %get-tuple-element.21), channel_id=1, source_target_pairs={{0,1},{2,3},{4,5},{6,7},{8,9},{10,11},{12,13},{14,15},{16,17},{18,... | collective-permute-start | bytes 1263176 | tf_op jit(solution)/shard_map/ppermute | solution.py:14
  252.3 4.9 %collective-permute-done.5 = f32[3,1,34,1032]{3,2,1,0:T(8,128)} collective-permute-done((f32[3,1,34,1032]{3,2,1,0:T(8,128)}, f32[3,1,34,1032]{3,2,1,0:T(8,128)}, u32[]{:S(2)}, u32[]{:S(2)}) %collective-permute-start.5) | collective-permute-done | bytes 421088 | tf_op jit(solution)/shard_map/ppermute | solution.py:17
  263.9 4.3 %collective-permute-start.6 = (f32[3,3,1,1032]{3,2,1,0:T(1,128)S(1)}, f32[3,3,1,1032]{3,2,1,0:T(1,128)S(1)}, u32[]{:S(2)}, u32[]{:S(2)}) collective-permute-start(f32[3,3,1,1032]{3,2,1,0:T(1,128)S(1)} %get-tuple-element.27), channel_id=1, source_target_pairs={{0,4},{4,8},{8,12},{12,16},{16,20},{20,24},{24,28},{1,5},{5,9},{9,... | collective-permute-start | bytes 111464 | tf_op jit(solution)/shard_map/ppermute | solution.py:14
  277.1 8.5 %collective-permute-done.8 = f32[3,1,34,1032]{3,2,1,0:T(8,128)S(1)} collective-permute-done((f32[3,1,34,1032]{3,2,1,0:T(8,128)S(1)}, f32[3,1,34,1032]{3,2,1,0:T(8,128)S(1)}, u32[]{:S(2)}, u32[]{:S(2)}) %collective-permute-start.8) | collective-permute-done | bytes 421088 | tf_op jit(solution)/shard_map/ppermute | solution.py:14
  285.6 4.1 %collective-permute-done.9 = f32[3,1,34,1032]{3,2,1,0:T(8,128)S(1)} collective-permute-done((f32[3,1,34,1032]{3,2,1,0:T(8,128)S(1)}, f32[3,1,34,1032]{3,2,1,0:T(8,128)S(1)}, u32[]{:S(2)}, u32[]{:S(2)}) %collective-permute-start.9) | collective-permute-done | bytes 421088 | tf_op jit(solution)/shard_map/ppermute | solution.py:17
  299.2 4.1 %collective-permute-done.11 = f32[3,3,1,1032]{3,2,1,0:T(1,128)S(1)} collective-permute-done((f32[3,3,1,1032]{3,2,1,0:T(1,128)S(1)}, f32[3,3,1,1032]{3,2,1,0:T(1,128)S(1)}, u32[]{:S(2)}, u32[]{:S(2)}) %collective-permute-start.11) | collective-permute-done | bytes 37184 | tf_op jit(solution)/shard_map/ppermute | solution.py:17
  306.2 6.1 %collective-permute-done.12 = f32[3,1,34,1032]{3,2,1,0:T(8,128)S(1)} collective-permute-done((f32[3,1,34,1032]{3,2,1,0:T(8,128)S(1)}, f32[3,1,34,1032]{3,2,1,0:T(8,128)S(1)}, u32[]{:S(2)}, u32[]{:S(2)}) %collective-permute-start.12) | collective-permute-done | bytes 421088 | tf_op jit(solution)/shard_map/ppermute | solution.py:14
  312.3 4.1 %collective-permute-done.13 = f32[3,1,34,1032]{3,2,1,0:T(8,128)S(1)} collective-permute-done((f32[3,1,34,1032]{3,2,1,0:T(8,128)S(1)}, f32[3,1,34,1032]{3,2,1,0:T(8,128)S(1)}, u32[]{:S(2)}, u32[]{:S(2)}) %collective-permute-start.13) | collective-permute-done | bytes 421088 | tf_op jit(solution)/shard_map/ppermute | solution.py:17
  320.7 4.3 %collective-permute-start.14 = (f32[3,3,1,1032]{3,2,1,0:T(1,128)S(1)}, f32[3,3,1,1032]{3,2,1,0:T(1,128)S(1)}, u32[]{:S(2)}, u32[]{:S(2)}) collective-permute-start(f32[3,3,1,1032]{3,2,1,0:T(1,128)S(1)} %get-tuple-element.23), channel_id=1, source_target_pairs={{0,4},{4,8},{8,12},{12,16},{16,20},{20,24},{24,28},{1,5},{5,9},{9,... | collective-permute-start | bytes 111464 | tf_op jit(solution)/shard_map/ppermute | solution.py:14
  326.7 4.2 %collective-permute-done.15 = f32[3,3,1,1032]{3,2,1,0:T(1,128)S(1)} collective-permute-done((f32[3,3,1,1032]{3,2,1,0:T(1,128)S(1)}, f32[3,3,1,1032]{3,2,1,0:T(1,128)S(1)}, u32[]{:S(2)}, u32[]{:S(2)}) %collective-permute-start.15) | collective-permute-done | bytes 37184 | tf_op jit(solution)/shard_map/ppermute | solution.py:17
  334.1 5.4 %collective-permute-done.16 = f32[3,1,34,1032]{3,2,1,0:T(8,128)S(1)} collective-permute-done((f32[3,1,34,1032]{3,2,1,0:T(8,128)S(1)}, f32[3,1,34,1032]{3,2,1,0:T(8,128)S(1)}, u32[]{:S(2)}, u32[]{:S(2)}) %collective-permute-start.16) | collective-permute-done | bytes 421088 | tf_op jit(solution)/shard_map/ppermute | solution.py:14
  339.5 4.4 %collective-permute-done.17 = f32[3,1,34,1032]{3,2,1,0:T(8,128)S(1)} collective-permute-done((f32[3,1,34,1032]{3,2,1,0:T(8,128)S(1)}, f32[3,1,34,1032]{3,2,1,0:T(8,128)S(1)}, u32[]{:S(2)}, u32[]{:S(2)}) %collective-permute-start.17) | collective-permute-done | bytes 421088 | tf_op jit(solution)/shard_map/ppermute | solution.py:17
  (90 shorter events, 70.3 us)
Async XLA Ops:
  6.5 78.5 %all-gather.3.cloned.1.call-start = ((), (), s32[]{:S(2)}) async-start(), calls=%async_computation.2 | async-start | bytes 4718592 | tf_op jit(solution)/shard_map/all_gather | solution.py:54
  8.6 96.3 %all-gather.5.cloned.1.call-start = ((), (), s32[]{:S(2)}) async-start(), calls=%async_computation.3 | async-start | bytes 12582912 | tf_op jit(solution)/shard_map/all_gather | solution.py:57
  85.0 20.0 %copy-start.10 = (bf16[2,3,32,2048]{3,2,1,0:T(8,128)(2,1)S(1)}, bf16[2,3,32,2048]{3,2,1,0:T(8,128)(2,1)}, u32[]{:S(2)}) copy-start(bf16[2,3,32,2048]{3,2,1,0:T(8,128)(2,1)} %param.6) | copy-start | bytes 2359300
  120.0 47.8 %all-to-all-start = ((bf16[8,2,24576]{2,1,0:T(2,128)(2,1)}), bf16[8,2,24576]{2,1,0:T(2,128)(2,1)S(1)}, u32[]{:S(2)}, u32[]{:S(2)}) async-start(bf16[8,2,24576]{2,1,0:T(2,128)(2,1)} %reshape.16), calls=%async_computation | async-start | bytes 1572864 | tf_op jit(solution)/shard_map/all_to_all | solution.py:65
  125.9 99.7 %all-reduce.8.cloned.1.call-start = ((), (), s32[]{:S(2)}) async-start(), calls=%async_computation.4 | async-start | bytes 4718592 | tf_op jit(solution)/shard_map/psum | solution.py:75
  205.9 37.4 %copy-start.6 = (f32[5,3,32,1024]{3,2,1,0:T(8,128)}, f32[5,3,32,1024]{3,2,1,0:T(8,128)S(1)}, u32[]{:S(2)}) copy-start(f32[5,3,32,1024]{3,2,1,0:T(8,128)S(1)} %constant_dynamic-update-slice_fusion) | copy-start | bytes 5898244
  227.1 5.4 %collective-permute-start.2 = (f32[3,3,1,1032]{3,2,1,0:T(1,128)S(1)}, f32[3,3,1,1032]{3,2,1,0:T(1,128)S(1)}, u32[]{:S(2)}, u32[]{:S(2)}) collective-permute-start(f32[3,3,1,1032]{3,2,1,0:T(1,128)S(1)} %get-tuple-element.5), channel_id=1, source_target_pairs={{0,4},{4,8},{8,12},{12,16},{16,20},{20,24},{24,28},{1,5},{5,9},{9,... | collective-permute-start | bytes 111464 | tf_op jit(solution)/shard_map/ppermute | solution.py:14
  230.7 5.9 %collective-permute-start.3 = (f32[3,3,1,1032]{3,2,1,0:T(1,128)S(1)}, f32[3,3,1,1032]{3,2,1,0:T(1,128)S(1)}, u32[]{:S(2)}, u32[]{:S(2)}) collective-permute-start(f32[3,3,1,1032]{3,2,1,0:T(1,128)S(1)} %get-tuple-element.6), channel_id=1, source_target_pairs={{4,0},{8,4},{12,8},{16,12},{20,16},{24,20},{28,24},{5,1},{9,5},{13... | collective-permute-start | bytes 111464 | tf_op jit(solution)/shard_map/ppermute | solution.py:17
  237.8 14.5 %collective-permute-start.4 = (f32[3,1,34,1032]{3,2,1,0:T(8,128)}, f32[3,1,34,1032]{3,2,1,0:T(8,128)}, u32[]{:S(2)}, u32[]{:S(2)}) collective-permute-start(f32[3,1,34,1032]{3,2,1,0:T(8,128)} %get-tuple-element.21), channel_id=1, source_target_pairs={{0,1},{2,3},{4,5},{6,7},{8,9},{10,11},{12,13},{14,15},{16,17},{18,... | collective-permute-start | bytes 1263176 | tf_op jit(solution)/shard_map/ppermute | solution.py:14
  241.9 15.2 %collective-permute-start.5 = (f32[3,1,34,1032]{3,2,1,0:T(8,128)}, f32[3,1,34,1032]{3,2,1,0:T(8,128)}, u32[]{:S(2)}, u32[]{:S(2)}) collective-permute-start(f32[3,1,34,1032]{3,2,1,0:T(8,128)} %get-tuple-element.22), channel_id=1, source_target_pairs={{1,0},{3,2},{5,4},{7,6},{9,8},{11,10},{13,12},{15,14},{17,16},{19,... | collective-permute-start | bytes 1263176 | tf_op jit(solution)/shard_map/ppermute | solution.py:17
  243.4 2.8 collective-permute-start
  244.7 3.4 collective-permute-start.1
  263.9 6.1 %collective-permute-start.6 = (f32[3,3,1,1032]{3,2,1,0:T(1,128)S(1)}, f32[3,3,1,1032]{3,2,1,0:T(1,128)S(1)}, u32[]{:S(2)}, u32[]{:S(2)}) collective-permute-start(f32[3,3,1,1032]{3,2,1,0:T(1,128)S(1)} %get-tuple-element.27), channel_id=1, source_target_pairs={{0,4},{4,8},{8,12},{12,16},{16,20},{20,24},{24,28},{1,5},{5,9},{9,... | collective-permute-start | bytes 111464 | tf_op jit(solution)/shard_map/ppermute | solution.py:14
  268.2 5.9 %collective-permute-start.7 = (f32[3,3,1,1032]{3,2,1,0:T(1,128)S(1)}, f32[3,3,1,1032]{3,2,1,0:T(1,128)S(1)}, u32[]{:S(2)}, u32[]{:S(2)}) collective-permute-start(f32[3,3,1,1032]{3,2,1,0:T(1,128)S(1)} %get-tuple-element.28), channel_id=1, source_target_pairs={{4,0},{8,4},{12,8},{16,12},{20,16},{24,20},{28,24},{5,1},{9,5},{13... | collective-permute-start | bytes 111464 | tf_op jit(solution)/shard_map/ppermute | solution.py:17
  274.3 11.3 %collective-permute-start.8 = (f32[3,1,34,1032]{3,2,1,0:T(8,128)S(1)}, f32[3,1,34,1032]{3,2,1,0:T(8,128)S(1)}, u32[]{:S(2)}, u32[]{:S(2)}) collective-permute-start(f32[3,1,34,1032]{3,2,1,0:T(8,128)S(1)} %get-tuple-element.19), channel_id=1, source_target_pairs={{0,1},{2,3},{4,5},{6,7},{8,9},{10,11},{12,13},{14,15},{16,17},{18,... | collective-permute-start | bytes 1263176 | tf_op jit(solution)/shard_map/ppermute | solution.py:14
  275.8 14.0 %collective-permute-start.9 = (f32[3,1,34,1032]{3,2,1,0:T(8,128)S(1)}, f32[3,1,34,1032]{3,2,1,0:T(8,128)S(1)}, u32[]{:S(2)}, u32[]{:S(2)}) collective-permute-start(f32[3,1,34,1032]{3,2,1,0:T(8,128)S(1)} %get-tuple-element.20), channel_id=1, source_target_pairs={{1,0},{3,2},{5,4},{7,6},{9,8},{11,10},{13,12},{15,14},{17,16},{19,... | collective-permute-start | bytes 1263176 | tf_op jit(solution)/shard_map/ppermute | solution.py:17
  294.0 5.2 %collective-permute-start.10 = (f32[3,3,1,1032]{3,2,1,0:T(1,128)S(1)}, f32[3,3,1,1032]{3,2,1,0:T(1,128)S(1)}, u32[]{:S(2)}, u32[]{:S(2)}) collective-permute-start(f32[3,3,1,1032]{3,2,1,0:T(1,128)S(1)} %get-tuple-element.25), channel_id=1, source_target_pairs={{0,4},{4,8},{8,12},{12,16},{16,20},{20,24},{24,28},{1,5},{5,9},{9,... | collective-permute-start | bytes 111464 | tf_op jit(solution)/shard_map/ppermute | solution.py:14
  297.4 5.9 %collective-permute-start.11 = (f32[3,3,1,1032]{3,2,1,0:T(1,128)S(1)}, f32[3,3,1,1032]{3,2,1,0:T(1,128)S(1)}, u32[]{:S(2)}, u32[]{:S(2)}) collective-permute-start(f32[3,3,1,1032]{3,2,1,0:T(1,128)S(1)} %get-tuple-element.26), channel_id=1, source_target_pairs={{4,0},{8,4},{12,8},{16,12},{20,16},{24,20},{28,24},{5,1},{9,5},{13... | collective-permute-start | bytes 111464 | tf_op jit(solution)/shard_map/ppermute | solution.py:17
  303.4 8.9 %collective-permute-start.12 = (f32[3,1,34,1032]{3,2,1,0:T(8,128)S(1)}, f32[3,1,34,1032]{3,2,1,0:T(8,128)S(1)}, u32[]{:S(2)}, u32[]{:S(2)}) collective-permute-start(f32[3,1,34,1032]{3,2,1,0:T(8,128)S(1)} %get-tuple-element.17), channel_id=1, source_target_pairs={{0,1},{2,3},{4,5},{6,7},{8,9},{10,11},{12,13},{14,15},{16,17},{18,... | collective-permute-start | bytes 1263176 | tf_op jit(solution)/shard_map/ppermute | solution.py:14
  304.9 11.5 %collective-permute-start.13 = (f32[3,1,34,1032]{3,2,1,0:T(8,128)S(1)}, f32[3,1,34,1032]{3,2,1,0:T(8,128)S(1)}, u32[]{:S(2)}, u32[]{:S(2)}) collective-permute-start(f32[3,1,34,1032]{3,2,1,0:T(8,128)S(1)} %get-tuple-element.18), channel_id=1, source_target_pairs={{1,0},{3,2},{5,4},{7,6},{9,8},{11,10},{13,12},{15,14},{17,16},{19,... | collective-permute-start | bytes 1263176 | tf_op jit(solution)/shard_map/ppermute | solution.py:17
  320.7 6.0 %collective-permute-start.14 = (f32[3,3,1,1032]{3,2,1,0:T(1,128)S(1)}, f32[3,3,1,1032]{3,2,1,0:T(1,128)S(1)}, u32[]{:S(2)}, u32[]{:S(2)}) collective-permute-start(f32[3,3,1,1032]{3,2,1,0:T(1,128)S(1)} %get-tuple-element.23), channel_id=1, source_target_pairs={{0,4},{4,8},{8,12},{12,16},{16,20},{20,24},{24,28},{1,5},{5,9},{9,... | collective-permute-start | bytes 111464 | tf_op jit(solution)/shard_map/ppermute | solution.py:14
  325.1 5.9 %collective-permute-start.15 = (f32[3,3,1,1032]{3,2,1,0:T(1,128)S(1)}, f32[3,3,1,1032]{3,2,1,0:T(1,128)S(1)}, u32[]{:S(2)}, u32[]{:S(2)}) collective-permute-start(f32[3,3,1,1032]{3,2,1,0:T(1,128)S(1)} %get-tuple-element.24), channel_id=1, source_target_pairs={{4,0},{8,4},{12,8},{16,12},{20,16},{24,20},{28,24},{5,1},{9,5},{13... | collective-permute-start | bytes 111464 | tf_op jit(solution)/shard_map/ppermute | solution.py:17
  331.1 8.4 %collective-permute-start.16 = (f32[3,1,34,1032]{3,2,1,0:T(8,128)S(1)}, f32[3,1,34,1032]{3,2,1,0:T(8,128)S(1)}, u32[]{:S(2)}, u32[]{:S(2)}) collective-permute-start(f32[3,1,34,1032]{3,2,1,0:T(8,128)S(1)} %get-tuple-element.15), channel_id=1, source_target_pairs={{0,1},{2,3},{4,5},{6,7},{8,9},{10,11},{12,13},{14,15},{16,17},{18,... | collective-permute-start | bytes 1263176 | tf_op jit(solution)/shard_map/ppermute | solution.py:14
  332.6 11.4 %collective-permute-start.17 = (f32[3,1,34,1032]{3,2,1,0:T(8,128)S(1)}, f32[3,1,34,1032]{3,2,1,0:T(8,128)S(1)}, u32[]{:S(2)}, u32[]{:S(2)}) collective-permute-start(f32[3,1,34,1032]{3,2,1,0:T(8,128)S(1)} %get-tuple-element.16), channel_id=1, source_target_pairs={{1,0},{3,2},{5,4},{7,6},{9,8},{11,10},{13,12},{15,14},{17,16},{19,... | collective-permute-start | bytes 1263176 | tf_op jit(solution)/shard_map/ppermute | solution.py:17
  (9 other events, 39.4 us)
Sparse Core Ops, SparseCore 0:
  9.5 75.4 all-gather.2
  86.5 18.3 all-gather.4
  204.4 21.1 all-reduce.7
where the time goes:
time: 357 us; the launch traced here: 356 us
  waiting for transfers between devices  174 us (49%)
  blocking collectives  64.2 us (18%)
  starting transfers between devices  43.5 us (12%)
  local copies, waits for them, and re-layouts  30.2 us (8%)
  other arithmetic  25.1 us (7%)
  between operations  13.6 us (4%)
  matrix products  5.59 us (2%)
    all_gather x1, waiting for transfers between devices, on_device(): column_block = lax.all_gather(own_block, 'row', axis=0, tiled=True)  76.3 us
    all_gather x1, blocking collectives, on_device(): row_whole = lax.all_gather(row_taper, 'row', axis=0, tiled=True)  41.8 us
    ppermute x9, waiting for transfers between devices, extended(): lax.ppermute(lax.slice_in_dim(block, 0, width, axis=dim), axis, backward)  36.1 us
    ppermute x9, starting transfers between devices, extended(): lax.ppermute(lax.slice_in_dim(block, block.shape[dim] - width, None, axis...  25.5 us
    all_to_all x1, blocking collectives, on_device(): lax.all_to_all(tapered.astype(jnp.bfloat16), 'row', split_axis=1, concat_...  22.4 us
    ppermute x9, waiting for transfers between devices, extended(): lax.ppermute(lax.slice_in_dim(block, block.shape[dim] - width, None, axis...  21.8 us
    all_gather x1, waiting for transfers between devices, on_device(): lax.all_gather(column_block, 'mem', axis=1, tiled=True)  19.9 us
    psum x1, waiting for transfers between devices, on_device(): summed = lax.psum(weighted, 'mem')  19.7 us
  transfers between devices with their start and end apart: 22, of which 19 were waited for; matrix products, arithmetic and copies ran while one was open for 2% of the time, Pallas kernels for 0%

commit v1 on v0

--- a/solution.py
+++ b/solution.py
@@ -4,6 +4,12 @@
 from jax.sharding import PartitionSpec as P
 
 STEPS = 4
+
+
+def laid_out(tiles, dim):
+    tiles = jnp.moveaxis(tiles, 0, dim)
+    shape = tiles.shape
+    return tiles.reshape(*shape[:dim], shape[dim] * shape[dim + 1], *shape[dim + 2 :])
 
 
 def extended(block, sides, width):
@@ -51,7 +57,19 @@
     own_block = lax.dynamic_slice_in_dim(
         column_taper, lax.axis_index("mem") * block_width, block_width, 1
     )
-    column_block = lax.all_gather(own_block, "row", axis=0, tiled=True)
+    count_2 = lax.axis_size("row")
+    pairs = [(i_2, (i_2 + 1) % count_2) for i_2 in range(count_2)]
+    back = [(b, a) for a, b in pairs]
+    lower, upper = ([], [])
+    for step in range(count_2 - 1):
+        if step % 2 == 0:
+            lower.append(lax.ppermute(lower[-1] if lower else own_block, "row", pairs))
+        else:
+            upper.append(lax.ppermute(upper[-1] if upper else own_block, "row", back))
+    blocks = jnp.stack([*lower[::-1], own_block, *upper])
+    shift = lax.axis_index("row") - len(lower)
+    blocks = blocks[(jnp.arange(count_2) - shift) % count_2]
+    column_block = laid_out(blocks, 0)
     first_pass = jnp.dot(
         flattened,
         lax.all_gather(column_block, "mem", axis=1, tiled=True),

time: 357 us -> 380 us (1.064)
  starting transfers between devices: 43.5 us -> 82.6 us
  waiting for transfers between devices: 174 us -> 145 us
  local copies, waits for them, and re-layouts: 30.2 us -> 42.9 us
    all_gather x1 -> x0, waiting for transfers between devices: 76.3 us -> none  [on_device(): column_block = lax.all_gather(own_block, 'row', axis=0, tiled=True)]
    ppermute x0 -> x7, waiting for transfers between devices: none -> 49.7 us  [the longest x4 49.7 us: on_device(): lower.append(lax.ppermute(lower[-1] if lower else own_block, 'row', pairs))]
    ppermute x0 -> x7, starting transfers between devices: none -> 38.4 us  [the longest x3 30.4 us: on_device(): upper.append(lax.ppermute(upper[-1] if upper else own_block, 'row', back))]
    unnamed x25 -> x32, local copies, waits for them, and re-layouts: 14 us -> 19.8 us
    gather x0 -> x1, local copies, waits for them, and re-layouts: none -> 5.05 us  [on_device(): blocks = blocks[(jnp.arange(count_2) - shift) % count_2]]
  transfers between devices with their start and end apart: 22 -> 28, of which waited for: 19 -> 22; matrix products, arithmetic and copies ran while one was open for 2% -> 4% of each run, Pallas kernels for 0% -> 0%
where the time goes in v1:
time: 380 us; the launch traced here: 379 us
  waiting for transfers between devices  145 us (38%)
  starting transfers between devices  82.6 us (22%)
  blocking collectives  64.2 us (17%)
  local copies, waits for them, and re-layouts  42.9 us (11%)
  other arithmetic  24.7 us (6%)
  between operations  13.9 us (4%)
  matrix products  5.59 us (1%)
    ppermute x4, waiting for transfers between devices, on_device(): lower.append(lax.ppermute(lower[-1] if lower else own_block, 'row', pairs))  49.7 us
    all_gather x1, blocking collectives, on_device(): row_whole = lax.all_gather(row_taper, 'row', axis=0, tiled=True)  41.8 us
    ppermute x9, waiting for transfers between devices, extended(): lax.ppermute(lax.slice_in_dim(block, 0, width, axis=dim), axis, backward)  32.4 us
    ppermute x3, starting transfers between devices, on_device(): upper.append(lax.ppermute(upper[-1] if upper else own_block, 'row', back))  30.4 us
    ppermute x9, starting transfers between devices, extended(): lax.ppermute(lax.slice_in_dim(block, block.shape[dim] - width, None, axis...  26.2 us
    ppermute x9, waiting for transfers between devices, extended(): lax.ppermute(lax.slice_in_dim(block, block.shape[dim] - width, None, axis...  24.7 us
    all_to_all x1, blocking collectives, on_device(): lax.all_to_all(tapered.astype(jnp.bfloat16), 'row', split_axis=1, concat_...  22.4 us
    unnamed x32, local copies, waits for them, and re-layouts  19.8 us
  transfers between devices with their start and end apart: 28, of which 22 were waited for; matrix products, arithmetic and copies ran while one was open for 4% of the time, Pallas kernels for 0%

profile of v1, /device:TPU:0, one launch (start us, length us, event | category | flops | bytes accessed | tf_op | source)
XLA Modules:
  0.0 378.9 jit_solution(13636920325170489562)
XLA Ops:
  10.7 15.0 %collective-permute-done = bf16[256,1024]{1,0:T(8,128)(2,1)S(1)} collective-permute-done((bf16[256,1024]{1,0:T(8,128)(2,1)S(1)}, bf16[256,1024]{1,0:T(8,128)(2,1)S(1)}, u32[]{:S(2)}, u32[]{:S(2)}) %collective-permute-start) | collective-permute-done | bytes 524320 | tf_op jit(solution)/shard_map/ppermute | solution.py:66
  25.7 4.7 %collective-permute-start.4 = (bf16[256,1024]{1,0:T(8,128)(2,1)S(1)}, bf16[256,1024]{1,0:T(8,128)(2,1)S(1)}, u32[]{:S(2)}, u32[]{:S(2)}) collective-permute-start(bf16[256,1024]{1,0:T(8,128)(2,1)S(1)} %constant_dynamic-slice_fusion), channel_id=1, source_target_pairs={{4,0},{8,4},{12,8},{16,12},{20,16},{24,20},{28,24},{0,28},{5,1},{9... | collective-permute-start | bytes 1572872 | tf_op jit(solution)/shard_map/ppermute | solution.py:68
  30.4 17.4 %collective-permute-done.1 = bf16[256,1024]{1,0:T(8,128)(2,1)S(1)} collective-permute-done((bf16[256,1024]{1,0:T(8,128)(2,1)S(1)}, bf16[256,1024]{1,0:T(8,128)(2,1)S(1)}, u32[]{:S(2)}, u32[]{:S(2)}) %collective-permute-start.1) | collective-permute-done | bytes 524320 | tf_op jit(solution)/shard_map/ppermute | solution.py:66
  50.3 12.3 %collective-permute-start.5 = (bf16[256,1024]{1,0:T(8,128)(2,1)S(1)}, bf16[256,1024]{1,0:T(8,128)(2,1)S(1)}, u32[]{:S(2)}, u32[]{:S(2)}) collective-permute-start(bf16[256,1024]{1,0:T(8,128)(2,1)S(1)} %collective-permute-done.4), channel_id=1, source_target_pairs={{4,0},{8,4},{12,8},{16,12},{20,16},{24,20},{28,24},{0,28},{5,1},{9... | collective-permute-start | bytes 1572872 | tf_op jit(solution)/shard_map/ppermute | solution.py:68
  62.5 9.1 %collective-permute-done.2 = bf16[256,1024]{1,0:T(8,128)(2,1)S(1)} collective-permute-done((bf16[256,1024]{1,0:T(8,128)(2,1)S(1)}, bf16[256,1024]{1,0:T(8,128)(2,1)S(1)}, u32[]{:S(2)}, u32[]{:S(2)}) %collective-permute-start.2) | collective-permute-done | bytes 524320 | tf_op jit(solution)/shard_map/ppermute | solution.py:66
  74.2 13.4 %collective-permute-start.6 = (bf16[256,1024]{1,0:T(8,128)(2,1)S(1)}, bf16[256,1024]{1,0:T(8,128)(2,1)S(1)}, u32[]{:S(2)}, u32[]{:S(2)}) collective-permute-start(bf16[256,1024]{1,0:T(8,128)(2,1)S(1)} %collective-permute-done.5), channel_id=1, source_target_pairs={{4,0},{8,4},{12,8},{16,12},{20,16},{24,20},{28,24},{0,28},{5,1},{9... | collective-permute-start | bytes 1572872 | tf_op jit(solution)/shard_map/ppermute | solution.py:68
  87.6 8.2 %collective-permute-done.3 = bf16[256,1024]{1,0:T(8,128)(2,1)} collective-permute-done((bf16[256,1024]{1,0:T(8,128)(2,1)S(1)}, bf16[256,1024]{1,0:T(8,128)(2,1)}, u32[]{:S(2)}, u32[]{:S(2)}) %collective-permute-start.3) | collective-permute-done | bytes 524320 | tf_op jit(solution)/shard_map/ppermute | solution.py:66
  103.6 5.1 %gather_fusion = bf16[8,256,1024]{2,1,0:T(8,128)(2,1)} fusion(bf16[8,256,1024]{2,1,0:T(8,128)(2,1)} %bitcast_dynamic-update-slice_fusion, s32[1024]{0:T(1024)S(1)} %pad_clamp_fusion), kind=kCustom, calls=%fused_computation | custom fusion | bytes 8388640 | tf_op jit(solution)/shard_map/gather | solution.py:71
  108.7 18.5 %all-gather.2.cloned.1.call-done = bf16[2048,2048]{1,0:T(8,128)(2,1)} async-done(((bf16[2048,1024]{1,0:T(8,128)(2,1)}), bf16[2048,2048]{1,0:T(8,128)(2,1)}) %all-gather.2.cloned.1.call-update) | async-done | bytes 8388624 | tf_op jit(solution)/shard_map/all_gather | solution.py:75
  127.3 5.2 %convolution_convert_fusion = bf16[2048,192]{0,1:T(8,128)(2,1)S(1)} fusion(bf16[192,2048]{1,0:T(8,128)(2,1)S(1)} %bitcast.60, bf16[2048,2048]{1,0:T(8,128)(2,1)} %all-gather.2.cloned.1.call-done), kind=kOutput, calls=%fused_computation.24 | convolution fusion | flops 1611005952 | bytes 9961472 | tf_op jit(solution)/shard_map/dot_general | solution.py:73
  136.6 5.7 %reshape.77 = bf16[8,2,24576]{2,1,0:T(2,128)(2,1)} reshape(bf16[2048,6,32]{2,1,0:T(8,128)(2,1)} %bitcast.61) | data formatting | bytes 1572864
  142.3 5.9 %all-to-all-start = ((bf16[8,2,24576]{2,1,0:T(2,128)(2,1)}), bf16[8,2,24576]{2,1,0:T(2,128)(2,1)S(1)}, u32[]{:S(2)}, u32[]{:S(2)}) async-start(bf16[8,2,24576]{2,1,0:T(2,128)(2,1)} %reshape.77), calls=%async_computation | async-start | bytes 1572864 | tf_op jit(solution)/shard_map/all_to_all | solution.py:83
  148.3 41.8 %all_gather.7 = bf16[256,256]{1,0:T(8,128)(2,1)S(1)} all-gather(bf16[32,256]{1,0:T(8,128)(2,1)S(1)} %copy-done.10), channel_id=1, replica_groups=mesh['row'=8,'mem'=2,'lev'=2] {'row'}, dimensions={0}, use_global_device_ids=true | all-gather | bytes 147456 | tf_op jit(solution)/shard_map/all_gather | solution.py:79
  199.7 22.4 %all_to_all.33 = bf16[6,256,256]{2,0,1:T(8,128)(2,1)S(1)} all-to-all(bf16[6,256,256]{2,0,1:T(8,128)(2,1)S(1)} %copy.19), channel_id=1, replica_groups=mesh['row'=8,'mem'=2,'lev'=2] {'row'}, dimensions={1} | all-to-all | bytes 1572864 | tf_op jit(solution)/shard_map/all_to_all | solution.py:86
  228.2 19.7 %all-reduce.8.cloned.1.call-done = f32[3,3,32,2048]{3,2,1,0:T(8,128)} async-done(((f32[3,3,32,2048]{3,2,1,0:T(8,128)}), f32[3,3,32,2048]{3,2,1,0:T(8,128)}) %all-reduce.8.cloned.1.call-update) | async-done | bytes 2359312 | tf_op jit(solution)/shard_map/psum | solution.py:93
  250.7 4.5 %collective-permute-start.9 = (f32[3,3,1,1032]{3,2,1,0:T(1,128)S(1)}, f32[3,3,1,1032]{3,2,1,0:T(1,128)S(1)}, u32[]{:S(2)}, u32[]{:S(2)}) collective-permute-start(f32[3,3,1,1032]{3,2,1,0:T(1,128)S(1)} %get-tuple-element.5), channel_id=1, source_target_pairs={{0,4},{4,8},{8,12},{12,16},{16,20},{20,24},{24,28},{1,5},{5,9},{9,... | collective-permute-start | bytes 111464 | tf_op jit(solution)/shard_map/ppermute | solution.py:20
  283.8 4.3 %collective-permute-start.13 = (f32[3,3,1,1032]{3,2,1,0:T(1,128)S(1)}, f32[3,3,1,1032]{3,2,1,0:T(1,128)S(1)}, u32[]{:S(2)}, u32[]{:S(2)}) collective-permute-start(f32[3,3,1,1032]{3,2,1,0:T(1,128)S(1)} %get-tuple-element.27), channel_id=1, source_target_pairs={{0,4},{4,8},{8,12},{12,16},{16,20},{20,24},{24,28},{1,5},{5,9},{9,... | collective-permute-start | bytes 111464 | tf_op jit(solution)/shard_map/ppermute | solution.py:20
  289.7 5.1 %collective-permute-done.14 = f32[3,3,1,1032]{3,2,1,0:T(1,128)S(1)} collective-permute-done((f32[3,3,1,1032]{3,2,1,0:T(1,128)S(1)}, f32[3,3,1,1032]{3,2,1,0:T(1,128)S(1)}, u32[]{:S(2)}, u32[]{:S(2)}) %collective-permute-start.14) | collective-permute-done | bytes 37184 | tf_op jit(solution)/shard_map/ppermute | solution.py:23
  297.7 9.5 %collective-permute-done.15 = f32[3,1,34,1032]{3,2,1,0:T(8,128)S(1)} collective-permute-done((f32[3,1,34,1032]{3,2,1,0:T(8,128)S(1)}, f32[3,1,34,1032]{3,2,1,0:T(8,128)S(1)}, u32[]{:S(2)}, u32[]{:S(2)}) %collective-permute-start.15) | collective-permute-done | bytes 421088 | tf_op jit(solution)/shard_map/ppermute | solution.py:20
  315.6 4.5 %collective-permute-start.17 = (f32[3,3,1,1032]{3,2,1,0:T(1,128)S(1)}, f32[3,3,1,1032]{3,2,1,0:T(1,128)S(1)}, u32[]{:S(2)}, u32[]{:S(2)}) collective-permute-start(f32[3,3,1,1032]{3,2,1,0:T(1,128)S(1)} %get-tuple-element.25), channel_id=1, source_target_pairs={{0,4},{4,8},{8,12},{12,16},{16,20},{20,24},{24,28},{1,5},{5,9},{9,... | collective-permute-start | bytes 111464 | tf_op jit(solution)/shard_map/ppermute | solution.py:20
  321.8 4.2 %collective-permute-done.18 = f32[3,3,1,1032]{3,2,1,0:T(1,128)S(1)} collective-permute-done((f32[3,3,1,1032]{3,2,1,0:T(1,128)S(1)}, f32[3,3,1,1032]{3,2,1,0:T(1,128)S(1)}, u32[]{:S(2)}, u32[]{:S(2)}) %collective-permute-start.18) | collective-permute-done | bytes 37184 | tf_op jit(solution)/shard_map/ppermute | solution.py:23
  329.0 6.7 %collective-permute-done.19 = f32[3,1,34,1032]{3,2,1,0:T(8,128)S(1)} collective-permute-done((f32[3,1,34,1032]{3,2,1,0:T(8,128)S(1)}, f32[3,1,34,1032]{3,2,1,0:T(8,128)S(1)}, u32[]{:S(2)}, u32[]{:S(2)}) %collective-permute-start.19) | collective-permute-done | bytes 421088 | tf_op jit(solution)/shard_map/ppermute | solution.py:20
  356.6 5.4 %collective-permute-done.23 = f32[3,1,34,1032]{3,2,1,0:T(8,128)S(1)} collective-permute-done((f32[3,1,34,1032]{3,2,1,0:T(8,128)S(1)}, f32[3,1,34,1032]{3,2,1,0:T(8,128)S(1)}, u32[]{:S(2)}, u32[]{:S(2)}) %collective-permute-start.23) | collective-permute-done | bytes 421088 | tf_op jit(solution)/shard_map/ppermute | solution.py:20
  362.1 4.4 %collective-permute-done.24 = f32[3,1,34,1032]{3,2,1,0:T(8,128)S(1)} collective-permute-done((f32[3,1,34,1032]{3,2,1,0:T(8,128)S(1)}, f32[3,1,34,1032]{3,2,1,0:T(8,128)S(1)}, u32[]{:S(2)}, u32[]{:S(2)}) %collective-permute-start.24) | collective-permute-done | bytes 421088 | tf_op jit(solution)/shard_map/ppermute | solution.py:23
  (112 shorter events, 111.9 us)
Async XLA Ops:
  6.5 120.7 %all-gather.2.cloned.1.call-start = ((), (), s32[]{:S(2)}) async-start(), calls=%async_computation.2 | async-start | bytes 12582912 | tf_op jit(solution)/shard_map/all_gather | solution.py:75
  7.7 18.0 %collective-permute-start = (bf16[256,1024]{1,0:T(8,128)(2,1)S(1)}, bf16[256,1024]{1,0:T(8,128)(2,1)S(1)}, u32[]{:S(2)}, u32[]{:S(2)}) collective-permute-start(bf16[256,1024]{1,0:T(8,128)(2,1)S(1)} %constant_dynamic-slice_fusion), channel_id=1, source_target_pairs={{0,4},{4,8},{8,12},{12,16},{16,20},{20,24},{24,28},{28,0},{1,5},{5... | collective-permute-start | bytes 1572872 | tf_op jit(solution)/shard_map/ppermute | solution.py:66
  25.7 22.1 %collective-permute-start.1 = (bf16[256,1024]{1,0:T(8,128)(2,1)S(1)}, bf16[256,1024]{1,0:T(8,128)(2,1)S(1)}, u32[]{:S(2)}, u32[]{:S(2)}) collective-permute-start(bf16[256,1024]{1,0:T(8,128)(2,1)S(1)} %collective-permute-done), channel_id=1, source_target_pairs={{0,4},{4,8},{8,12},{12,16},{16,20},{20,24},{24,28},{28,0},{1,5},{5... | collective-permute-start | bytes 1572872 | tf_op jit(solution)/shard_map/ppermute | solution.py:66
  25.7 24.6 %collective-permute-start.4 = (bf16[256,1024]{1,0:T(8,128)(2,1)S(1)}, bf16[256,1024]{1,0:T(8,128)(2,1)S(1)}, u32[]{:S(2)}, u32[]{:S(2)}) collective-permute-start(bf16[256,1024]{1,0:T(8,128)(2,1)S(1)} %constant_dynamic-slice_fusion), channel_id=1, source_target_pairs={{4,0},{8,4},{12,8},{16,12},{20,16},{24,20},{28,24},{0,28},{5,1},{9... | collective-permute-start | bytes 1572872 | tf_op jit(solution)/shard_map/ppermute | solution.py:68
  47.8 23.9 %collective-permute-start.2 = (bf16[256,1024]{1,0:T(8,128)(2,1)S(1)}, bf16[256,1024]{1,0:T(8,128)(2,1)S(1)}, u32[]{:S(2)}, u32[]{:S(2)}) collective-permute-start(bf16[256,1024]{1,0:T(8,128)(2,1)S(1)} %collective-permute-done.1), channel_id=1, source_target_pairs={{0,4},{4,8},{8,12},{12,16},{16,20},{20,24},{24,28},{28,0},{1,5},{5... | collective-permute-start | bytes 1572872 | tf_op jit(solution)/shard_map/ppermute | solution.py:66
  50.3 23.9 %collective-permute-start.5 = (bf16[256,1024]{1,0:T(8,128)(2,1)S(1)}, bf16[256,1024]{1,0:T(8,128)(2,1)S(1)}, u32[]{:S(2)}, u32[]{:S(2)}) collective-permute-start(bf16[256,1024]{1,0:T(8,128)(2,1)S(1)} %collective-permute-done.4), channel_id=1, source_target_pairs={{4,0},{8,4},{12,8},{16,12},{20,16},{24,20},{28,24},{0,28},{5,1},{9... | collective-permute-start | bytes 1572872 | tf_op jit(solution)/shard_map/ppermute | solution.py:68
  71.7 24.1 %collective-permute-start.3 = (bf16[256,1024]{1,0:T(8,128)(2,1)S(1)}, bf16[256,1024]{1,0:T(8,128)(2,1)}, u32[]{:S(2)}, u32[]{:S(2)}) collective-permute-start(bf16[256,1024]{1,0:T(8,128)(2,1)S(1)} %collective-permute-done.2), channel_id=1, source_target_pairs={{0,4},{4,8},{8,12},{12,16},{16,20},{20,24},{24,28},{28,0},{1,5},{5... | collective-permute-start | bytes 1572872 | tf_op jit(solution)/shard_map/ppermute | solution.py:66
  74.2 28.6 %collective-permute-start.6 = (bf16[256,1024]{1,0:T(8,128)(2,1)S(1)}, bf16[256,1024]{1,0:T(8,128)(2,1)S(1)}, u32[]{:S(2)}, u32[]{:S(2)}) collective-permute-start(bf16[256,1024]{1,0:T(8,128)(2,1)S(1)} %collective-permute-done.5), channel_id=1, source_target_pairs={{4,0},{8,4},{12,8},{16,12},{20,16},{24,20},{28,24},{0,28},{5,1},{9... | collective-permute-start | bytes 1572872 | tf_op jit(solution)/shard_map/ppermute | solution.py:68
  142.3 47.8 %all-to-all-start = ((bf16[8,2,24576]{2,1,0:T(2,128)(2,1)}), bf16[8,2,24576]{2,1,0:T(2,128)(2,1)S(1)}, u32[]{:S(2)}, u32[]{:S(2)}) async-start(bf16[8,2,24576]{2,1,0:T(2,128)(2,1)} %reshape.77), calls=%async_computation | async-start | bytes 1572864 | tf_op jit(solution)/shard_map/all_to_all | solution.py:83
  148.2 99.7 %all-reduce.8.cloned.1.call-start = ((), (), s32[]{:S(2)}) async-start(), calls=%async_computation.3 | async-start | bytes 4718592 | tf_op jit(solution)/shard_map/psum | solution.py:93
  249.4 6.3 %collective-permute-start.10 = (f32[3,3,1,1032]{3,2,1,0:T(1,128)S(1)}, f32[3,3,1,1032]{3,2,1,0:T(1,128)S(1)}, u32[]{:S(2)}, u32[]{:S(2)}) collective-permute-start(f32[3,3,1,1032]{3,2,1,0:T(1,128)S(1)} %get-tuple-element.6), channel_id=1, source_target_pairs={{4,0},{8,4},{12,8},{16,12},{20,16},{24,20},{28,24},{5,1},{9,5},{13... | collective-permute-start | bytes 111464 | tf_op jit(solution)/shard_map/ppermute | solution.py:23
  250.7 6.2 %collective-permute-start.9 = (f32[3,3,1,1032]{3,2,1,0:T(1,128)S(1)}, f32[3,3,1,1032]{3,2,1,0:T(1,128)S(1)}, u32[]{:S(2)}, u32[]{:S(2)}) collective-permute-start(f32[3,3,1,1032]{3,2,1,0:T(1,128)S(1)} %get-tuple-element.5), channel_id=1, source_target_pairs={{0,4},{4,8},{8,12},{12,16},{16,20},{20,24},{24,28},{1,5},{5,9},{9,... | collective-permute-start | bytes 111464 | tf_op jit(solution)/shard_map/ppermute | solution.py:20
  258.0 15.1 %collective-permute-start.11 = (f32[3,1,34,1032]{3,2,1,0:T(8,128)}, f32[3,1,34,1032]{3,2,1,0:T(8,128)S(1)}, u32[]{:S(2)}, u32[]{:S(2)}) collective-permute-start(f32[3,1,34,1032]{3,2,1,0:T(8,128)} %get-tuple-element.21), channel_id=1, source_target_pairs={{0,1},{2,3},{4,5},{6,7},{8,9},{10,11},{12,13},{14,15},{16,17},{18,... | collective-permute-start | bytes 1263176 | tf_op jit(solution)/shard_map/ppermute | solution.py:20
  261.7 15.6 %collective-permute-start.12 = (f32[3,1,34,1032]{3,2,1,0:T(8,128)}, f32[3,1,34,1032]{3,2,1,0:T(8,128)}, u32[]{:S(2)}, u32[]{:S(2)}) collective-permute-start(f32[3,1,34,1032]{3,2,1,0:T(8,128)} %get-tuple-element.22), channel_id=1, source_target_pairs={{1,0},{3,2},{5,4},{7,6},{9,8},{11,10},{13,12},{15,14},{17,16},{19,... | collective-permute-start | bytes 1263176 | tf_op jit(solution)/shard_map/ppermute | solution.py:23
  283.8 5.9 %collective-permute-start.13 = (f32[3,3,1,1032]{3,2,1,0:T(1,128)S(1)}, f32[3,3,1,1032]{3,2,1,0:T(1,128)S(1)}, u32[]{:S(2)}, u32[]{:S(2)}) collective-permute-start(f32[3,3,1,1032]{3,2,1,0:T(1,128)S(1)} %get-tuple-element.27), channel_id=1, source_target_pairs={{0,4},{4,8},{8,12},{12,16},{16,20},{20,24},{24,28},{1,5},{5,9},{9,... | collective-permute-start | bytes 111464 | tf_op jit(solution)/shard_map/ppermute | solution.py:20
  288.1 6.8 %collective-permute-start.14 = (f32[3,3,1,1032]{3,2,1,0:T(1,128)S(1)}, f32[3,3,1,1032]{3,2,1,0:T(1,128)S(1)}, u32[]{:S(2)}, u32[]{:S(2)}) collective-permute-start(f32[3,3,1,1032]{3,2,1,0:T(1,128)S(1)} %get-tuple-element.28), channel_id=1, source_target_pairs={{4,0},{8,4},{12,8},{16,12},{20,16},{24,20},{28,24},{5,1},{9,5},{13... | collective-permute-start | bytes 111464 | tf_op jit(solution)/shard_map/ppermute | solution.py:23
  295.0 12.3 %collective-permute-start.15 = (f32[3,1,34,1032]{3,2,1,0:T(8,128)S(1)}, f32[3,1,34,1032]{3,2,1,0:T(8,128)S(1)}, u32[]{:S(2)}, u32[]{:S(2)}) collective-permute-start(f32[3,1,34,1032]{3,2,1,0:T(8,128)S(1)} %get-tuple-element.19), channel_id=1, source_target_pairs={{0,1},{2,3},{4,5},{6,7},{8,9},{10,11},{12,13},{14,15},{16,17},{18,... | collective-permute-start | bytes 1263176 | tf_op jit(solution)/shard_map/ppermute | solution.py:20
  296.4 14.9 %collective-permute-start.16 = (f32[3,1,34,1032]{3,2,1,0:T(8,128)S(1)}, f32[3,1,34,1032]{3,2,1,0:T(8,128)S(1)}, u32[]{:S(2)}, u32[]{:S(2)}) collective-permute-start(f32[3,1,34,1032]{3,2,1,0:T(8,128)S(1)} %get-tuple-element.20), channel_id=1, source_target_pairs={{1,0},{3,2},{5,4},{7,6},{9,8},{11,10},{13,12},{15,14},{17,16},{19,... | collective-permute-start | bytes 1263176 | tf_op jit(solution)/shard_map/ppermute | solution.py:23
  315.6 6.2 %collective-permute-start.17 = (f32[3,3,1,1032]{3,2,1,0:T(1,128)S(1)}, f32[3,3,1,1032]{3,2,1,0:T(1,128)S(1)}, u32[]{:S(2)}, u32[]{:S(2)}) collective-permute-start(f32[3,3,1,1032]{3,2,1,0:T(1,128)S(1)} %get-tuple-element.25), channel_id=1, source_target_pairs={{0,4},{4,8},{8,12},{12,16},{16,20},{20,24},{24,28},{1,5},{5,9},{9,... | collective-permute-start | bytes 111464 | tf_op jit(solution)/shard_map/ppermute | solution.py:20
  320.2 5.9 %collective-permute-start.18 = (f32[3,3,1,1032]{3,2,1,0:T(1,128)S(1)}, f32[3,3,1,1032]{3,2,1,0:T(1,128)S(1)}, u32[]{:S(2)}, u32[]{:S(2)}) collective-permute-start(f32[3,3,1,1032]{3,2,1,0:T(1,128)S(1)} %get-tuple-element.26), channel_id=1, source_target_pairs={{4,0},{8,4},{12,8},{16,12},{20,16},{24,20},{28,24},{5,1},{9,5},{13... | collective-permute-start | bytes 111464 | tf_op jit(solution)/shard_map/ppermute | solution.py:23
  326.2 9.5 %collective-permute-start.19 = (f32[3,1,34,1032]{3,2,1,0:T(8,128)S(1)}, f32[3,1,34,1032]{3,2,1,0:T(8,128)S(1)}, u32[]{:S(2)}, u32[]{:S(2)}) collective-permute-start(f32[3,1,34,1032]{3,2,1,0:T(8,128)S(1)} %get-tuple-element.17), channel_id=1, source_target_pairs={{0,1},{2,3},{4,5},{6,7},{8,9},{10,11},{12,13},{14,15},{16,17},{18,... | collective-permute-start | bytes 1263176 | tf_op jit(solution)/shard_map/ppermute | solution.py:20
  327.7 12.2 %collective-permute-start.20 = (f32[3,1,34,1032]{3,2,1,0:T(8,128)S(1)}, f32[3,1,34,1032]{3,2,1,0:T(8,128)S(1)}, u32[]{:S(2)}, u32[]{:S(2)}) collective-permute-start(f32[3,1,34,1032]{3,2,1,0:T(8,128)S(1)} %get-tuple-element.18), channel_id=1, source_target_pairs={{1,0},{3,2},{5,4},{7,6},{9,8},{11,10},{13,12},{15,14},{17,16},{19,... | collective-permute-start | bytes 1263176 | tf_op jit(solution)/shard_map/ppermute | solution.py:23
  353.6 8.4 %collective-permute-start.23 = (f32[3,1,34,1032]{3,2,1,0:T(8,128)S(1)}, f32[3,1,34,1032]{3,2,1,0:T(8,128)S(1)}, u32[]{:S(2)}, u32[]{:S(2)}) collective-permute-start(f32[3,1,34,1032]{3,2,1,0:T(8,128)S(1)} %get-tuple-element.15), channel_id=1, source_target_pairs={{0,1},{2,3},{4,5},{6,7},{8,9},{10,11},{12,13},{14,15},{16,17},{18,... | collective-permute-start | bytes 1263176 | tf_op jit(solution)/shard_map/ppermute | solution.py:20
  355.1 11.4 %collective-permute-start.24 = (f32[3,1,34,1032]{3,2,1,0:T(8,128)S(1)}, f32[3,1,34,1032]{3,2,1,0:T(8,128)S(1)}, u32[]{:S(2)}, u32[]{:S(2)}) collective-permute-start(f32[3,1,34,1032]{3,2,1,0:T(8,128)S(1)} %get-tuple-element.16), channel_id=1, source_target_pairs={{1,0},{3,2},{5,4},{7,6},{9,8},{11,10},{13,12},{15,14},{17,16},{19,... | collective-permute-start | bytes 1263176 | tf_op jit(solution)/shard_map/ppermute | solution.py:23
  (15 other events, 211.2 us)
Sparse Core Ops, SparseCore 0:
  108.8 18.3 all-gather.1
  226.7 21.1 all-reduce.7
